TPU v7x, 32 devices: a whole 2x2x4 slice. The times are simulated.
32 devices in a mesh: sweep: 2 (over y), expert: 4 (over z), dp: 4 (over x, core).
Axes of the slice: x: 2, y: 2, z: 4, core: 2. Of those that a mesh axis runs over, the one named last changes fastest.
Arguments:
- tokens: bfloat16 [4096, 1536], P(('sweep', 'expert', 'dp')), parts along dimension 0, may hold values from -6 to 6
- expert_ids: int32 [4096, 8], P(('sweep', 'expert', 'dp')), parts along dimension 0, may hold values from 0 to 63, all different within a row; in each aligned block of 128 rows (0 to 127, 128 to 255, ...) at most 20 rows name the same one
- gate_weights: float32 [4096, 8], P(('sweep', 'expert', 'dp')), parts along dimension 0, may hold values from 0.1 to 0.6
- expert_in: bfloat16 [128, 1536, 768], P(('sweep', 'expert'), 'dp'), parts along dimension 0, may hold values from -0.15625 to 0.15625
- expert_out: bfloat16 [128, 768, 1536], P(('sweep', 'expert'), None, 'dp'), parts along dimension 0, may hold values from -0.21875 to 0.21875
- shared_in: bfloat16 [3072, 768], P(('sweep', 'dp')), parts along dimension 0, may hold values from -0.15625 to 0.15625
- shared_out: bfloat16 [1536, 1536], P('sweep', 'dp'), parts along dimension 0, may hold values from -0.21875 to 0.21875
Outputs:
- block_out: bfloat16 [4096, 1536], P(('sweep', 'expert', 'dp')), parts along dimension 0
There are 2 independent parts, one for each index of `sweep`. A program takes and returns all parts, laid end to end along the dimension named above; each array names one. Nothing has to cross between parts.
Inputs may be any that keep to these rules, and one draw needn't show every extreme that they name: `expert_ids`: each token names 8 different experts. In each aligned block of 128 tokens (the tokens of one device) no expert is named by more than 20 tokens; some blocks have an expert named by exactly 20.
All inputs are finite; a program needn't handle non-finite values.
Results may differ from a plain program's by a relative error of at most 0.0051.
Values may be sent and summed in bfloat16 or wider, within the bound.
A program may use at most 192 MiB of HBM per device.

v0:
```python
import jax
import jax.numpy as jnp
from jax import lax
from jax.sharding import PartitionSpec as P

CAP = 20


def layer_norm(tokens):
    values = tokens.astype(jnp.float32)
    center = values - jnp.mean(values, axis=-1, keepdims=True)
    spread = jnp.mean(center * center, axis=-1, keepdims=True)
    return (center * lax.rsqrt(spread + 1e-06)).astype(jnp.bfloat16)


def copy_slots(expert_ids, expert_count):
    expert_iota = jnp.arange(expert_count, dtype=jnp.int32)
    matches = (expert_ids[..., None] == expert_iota).astype(jnp.int32)
    per_token = jnp.sum(matches, axis=-2, dtype=jnp.int32)
    earlier = jnp.cumsum(per_token, axis=-2, dtype=jnp.int32) - per_token
    return jnp.sum(matches * earlier[..., None, :], axis=-1, dtype=jnp.int32)


def run_experts(shard_piece, weight_in, weight_out):
    pre_act = jnp.einsum(
        "gesd,edf->gesf", shard_piece, weight_in, preferred_element_type=jnp.float32
    )
    hidden = jax.nn.gelu(pre_act).astype(jnp.bfloat16)
    return jnp.einsum(
        "gesf,efd->gesd", hidden, weight_out, preferred_element_type=jnp.float32
    ).astype(jnp.bfloat16)


def per_device(tokens, expert_ids, gate_weights, expert_in, expert_out, shared_in, shared_out):
    row_count, model_width = tokens.shape
    pick_count = expert_ids.shape[1]
    local_count = expert_in.shape[0]
    group_count = lax.axis_size("expert")
    expert_total = local_count * group_count
    normed = layer_norm(tokens)
    full_in, full_out = (
        lax.all_gather(expert_in, "dp", axis=1, tiled=True),
        lax.all_gather(expert_out, "dp", axis=2, tiled=True),
    )
    slot_of = copy_slots(expert_ids, expert_total)
    positions = (expert_ids * CAP + slot_of).reshape(-1)
    copies = jnp.repeat(normed, pick_count, axis=0)
    outgoing = jnp.zeros((expert_total * CAP, model_width), jnp.bfloat16).at[positions].set(copies)
    outgoing = outgoing.reshape(group_count, local_count, CAP, model_width)
    received = lax.all_to_all(outgoing, "expert", split_axis=0, concat_axis=0, tiled=True)
    returned = lax.all_to_all(
        run_experts(received, full_in, full_out), "expert", split_axis=0, concat_axis=0, tiled=True
    )
    results = returned.reshape(expert_total * CAP, model_width)[positions].reshape(
        row_count, pick_count, model_width
    )
    routed = jnp.sum(results.astype(jnp.float32) * gate_weights[:, :, None], axis=1)
    shared_pre = jnp.dot(
        normed,
        lax.all_gather(shared_in, "dp", axis=0, tiled=True),
        preferred_element_type=jnp.float32,
    )
    shared_hidden = jax.nn.gelu(shared_pre).astype(jnp.bfloat16)
    shared_result = jnp.dot(
        shared_hidden,
        lax.all_gather(shared_out, "dp", axis=1, tiled=True),
        preferred_element_type=jnp.float32,
    )
    return (tokens.astype(jnp.float32) + shared_result + routed).astype(jnp.bfloat16)


def solution(mesh):
    placed = (
        P(("sweep", "expert", "dp"), None),
        P(("sweep", "expert", "dp"), None),
        P(("sweep", "expert", "dp"), None),
        P(("sweep", "expert"), "dp", None),
        P(("sweep", "expert"), None, "dp"),
        P(("sweep", "dp"), None),
        P("sweep", "dp"),
    )
    return jax.shard_map(
        per_device,
        mesh=mesh,
        in_specs=placed,
        out_specs=P(("sweep", "expert", "dp"), None),
        check_vma=False,
    )
```

profile of v0, /device:TPU:0, one launch (start us, length us, event | category | flops | bytes accessed | tf_op | source)
XLA Modules:
  0.0 624.6 jit_solution(13773395586247064220)
XLA Ops:
  6.5 0.7 all-gather.9.cloned.1.call-update
  7.3 0.7 all-gather.11.cloned.1.call-update
  8.1 0.1 copy.22
  8.2 0.2 reduce_window_sum.11
  8.4 0.1 copy.24
  8.4 0.1 select_reduce_fusion
  8.5 0.1 copy.25
  8.6 0.1 reshape.66
  8.7 0.1 convert_reduce_fusion
  8.9 0.3 fusion.29
  9.1 0.2 fusion.30
  9.4 8.1 %scatter_custom_fusion = bf16[1280,1536]{1,0:T(8,128)(2,1)} fusion(s32[1024]{0:T(1024)S(1)} %bitcast.27, bf16[]{:T(256)} %constant.6.clone.1, bf16[128,1536]{1,0:T(8,128)(2,1)S(1)} %fusion.30), kind=kCustom, calls=%fused_computation.19 | custom fusion | bytes 4325378 | tf_op jit(solution)/shard_map/scatter | solution.py:48
  17.5 7.5 %reshape.68 = bf16[4,16,20,1536]{3,2,1,0:T(8,128)(2,1)} reshape(bf16[1280,1536]{1,0:T(8,128)(2,1)} %scatter_custom_fusion) | data formatting | bytes 7864320 | tf_op jit(solution)/shard_map/reshape | solution.py:49
  24.9 6.8 %copy.26 = bf16[4,16,20,1536]{3,1,2,0:T(8,128)(2,1)} copy(bf16[4,16,20,1536]{3,2,1,0:T(8,128)(2,1)} %reshape.68) | data formatting | bytes 7864320 | tf_op jit(solution)/shard_map/reshape | solution.py:49
  31.7 7.1 %all-to-all-start = ((bf16[4,16,20,1536]{3,1,2,0:T(8,128)(2,1)}), bf16[4,16,20,1536]{3,1,2,0:T(8,128)(2,1)}, u32[]{:S(2)}, u32[]{:S(2)}) async-start(bf16[4,16,20,1536]{3,1,2,0:T(8,128)(2,1)} %copy.26), calls=%async_computation | async-start | bytes 7864320 | tf_op jit(solution)/shard_map/all_to_all | solution.py:50
  38.8 0.7 all-gather.5.cloned.1.call-update
  39.5 87.2 %all-to-all-done = bf16[4,16,20,1536]{3,1,2,0:T(8,128)(2,1)} async-done(((bf16[4,16,20,1536]{3,1,2,0:T(8,128)(2,1)}), bf16[4,16,20,1536]{3,1,2,0:T(8,128)(2,1)}, u32[]{:S(2)}, u32[]{:S(2)}) %all-to-all-start) | async-done | bytes 3932192 | tf_op jit(solution)/shard_map/all_to_all | solution.py:50
  126.8 112.0 %all-gather.9.cloned.1.call-done = bf16[16,1536,768]{2,1,0:T(8,128)(2,1)} async-done(((bf16[16,384,768]{2,1,0:T(8,128)(2,1)}), bf16[16,1536,768]{2,1,0:T(8,128)(2,1)}) %all-gather.9.cloned.1.call-update) | async-done | bytes 37748752 | tf_op jit(solution)/shard_map/all_gather | solution.py:42
  238.7 28.0 %fusion.2 = f32[16,4,20,768]{3,2,1,0:T(8,128)} fusion(bf16[16,1536,768]{2,1,0:T(8,128)(2,1)} %all-gather.9.cloned.1.call-done, bf16[4,16,20,1536]{3,1,2,0:T(8,128)(2,1)} %all-to-all-done), kind=kOutput, calls=%fused_computation.4 | convolution fusion | flops 3019898880 | bytes 45613056 | tf_op jit(solution)/shard_map/gesd,edf->gesf/dot_general | solution.py:25
  266.7 200.2 %all-gather.11.cloned.1.call-done = bf16[16,768,1536]{2,1,0:T(8,128)(2,1)} async-done(((bf16[16,768,384]{2,1,0:T(8,128)(2,1)}), bf16[16,768,1536]{2,1,0:T(8,128)(2,1)}) %all-gather.11.cloned.1.call-update) | async-done | bytes 37748752 | tf_op jit(solution)/shard_map/all_gather | solution.py:43
  466.9 19.8 %convert_bitcast_fusion = bf16[4,16,20,1536]{3,2,0,1:T(8,128)(2,1)} fusion(bf16[16,768,1536]{2,1,0:T(8,128)(2,1)} %all-gather.11.cloned.1.call-done, f32[16,4,20,768]{3,2,1,0:T(8,128)} %fusion.2), kind=kOutput, calls=%fused_computation.18 | convolution fusion | flops 3030712320 | bytes 45613056 | tf_op jit(solution)/shard_map/gesf,efd->gesd/dot_general | solution.py:29
  486.7 6.4 %copy.28 = bf16[4,16,20,1536]{3,1,2,0:T(8,128)(2,1)} copy(bf16[4,16,20,1536]{3,2,0,1:T(8,128)(2,1)} %convert_bitcast_fusion) | data formatting | bytes 7864320 | tf_op jit(solution)/shard_map/convert_element_type | solution.py:31
  493.1 5.0 all-to-all-start.1
  498.1 0.0 all-gather.7.cloned.1.call-start
  498.1 0.5 all-gather.7.cloned.1.call-update
  498.7 0.7 copy.30
  499.4 87.0 %all-to-all-done.1 = bf16[4,16,20,1536]{3,1,2,0:T(8,128)(2,1)} async-done(((bf16[4,16,20,1536]{3,1,2,0:T(8,128)(2,1)}), bf16[4,16,20,1536]{3,1,2,0:T(8,128)(2,1)}, u32[]{:S(2)}, u32[]{:S(2)}) %all-to-all-start.1) | async-done | bytes 3932192 | tf_op jit(solution)/shard_map/all_to_all | solution.py:51
  586.4 6.5 %copy.29 = bf16[4,16,20,1536]{3,2,1,0:T(8,128)(2,1)} copy(bf16[4,16,20,1536]{3,1,2,0:T(8,128)(2,1)} %all-to-all-done.1) | data formatting | bytes 7864320 | tf_op jit(solution)/shard_map/all_to_all | solution.py:51
  592.9 6.9 %reshape.69 = bf16[1280,1536]{1,0:T(8,128)(2,1)} reshape(bf16[4,16,20,1536]{3,2,1,0:T(8,128)(2,1)} %copy.29) | data formatting | bytes 7864320 | tf_op jit(solution)/shard_map/reshape | solution.py:54
  599.8 9.3 %gather_fusion = bf16[1024,1536]{1,0:T(8,128)(2,1)S(1)} fusion(bf16[1280,1536]{1,0:T(8,128)(2,1)} %reshape.69, s32[1024]{0:T(1024)S(1)} %broadcast_clamp_fusion), kind=kCustom, calls=%fused_computation | custom fusion | bytes 6295552 | tf_op jit(solution)/shard_map/gather | solution.py:54
  609.1 4.5 fusion.4
  613.6 4.4 fusion.19
  (18 shorter events, 0.1 us)
Async XLA Ops:
  6.5 232.2 %all-gather.9.cloned.1.call-start = ((), (), s32[]{:S(2)}) async-start(), calls=%async_computation.4 | async-start | bytes 47185920 | tf_op jit(solution)/shard_map/all_gather | solution.py:42
  7.3 0.8 copy-start.1
  7.3 1.4 copy-start
  7.3 459.7 %all-gather.11.cloned.1.call-start = ((), (), s32[]{:S(2)}) async-start(), calls=%async_computation.5 | async-start | bytes 47185920 | tf_op jit(solution)/shard_map/all_gather | solution.py:43
  31.7 95.1 %all-to-all-start = ((bf16[4,16,20,1536]{3,1,2,0:T(8,128)(2,1)}), bf16[4,16,20,1536]{3,1,2,0:T(8,128)(2,1)}, u32[]{:S(2)}, u32[]{:S(2)}) async-start(bf16[4,16,20,1536]{3,1,2,0:T(8,128)(2,1)} %copy.26), calls=%async_computation | async-start | bytes 7864320 | tf_op jit(solution)/shard_map/all_to_all | solution.py:50
  38.8 574.8 %all-gather.5.cloned.1.call-start = ((), (), s32[]{:S(2)}) async-start(), calls=%async_computation.2 | async-start | bytes 2949120 | tf_op jit(solution)/shard_map/all_gather | solution.py:60
  493.1 5.5 copy-start.2
  493.1 93.3 %all-to-all-start.1 = ((bf16[4,16,20,1536]{3,1,2,0:T(8,128)(2,1)}), bf16[4,16,20,1536]{3,1,2,0:T(8,128)(2,1)}, u32[]{:S(2)}, u32[]{:S(2)}) async-start(bf16[4,16,20,1536]{3,1,2,0:T(8,128)(2,1)} %copy.28), calls=%async_computation.1 | async-start | bytes 7864320 | tf_op jit(solution)/shard_map/all_to_all | solution.py:51
  498.1 115.5 %all-gather.7.cloned.1.call-start = ((), (), s32[]{:S(2)}) async-start(), calls=%async_computation.3 | async-start | bytes 2949120 | tf_op jit(solution)/shard_map/all_gather | solution.py:66
Sparse Core Ops, SparseCore 0:
  8.9 229.7 all-gather.8
  240.3 226.6 all-gather.10
  468.5 24.0 all-gather.4
  500.2 24.4 all-gather.6
where the time goes:
time: 625 us
  waiting for transfers between devices  489 us (78%)
  local copies, waits for them, and re-layouts  52.5 us (8%)
  matrix products  52.2 us (8%)
  between operations  13.2 us (2%)
  starting transfers between devices  12.1 us (2%)
    all_gather x1, waiting for transfers between devices, per_device(): lax.all_gather(expert_out, 'dp', axis=2, tiled=True)  200 us
    all_gather x1, waiting for transfers between devices, per_device(): lax.all_gather(expert_in, 'dp', axis=1, tiled=True)  112 us
    all_to_all x1, waiting for transfers between devices, per_device(): lax.all_to_all(outgoing, 'expert', split_axis=0, concat_axis=0, tiled=True)  87.2 us
    all_to_all x1, waiting for transfers between devices, per_device(): lax.all_to_all(run_experts(received, full_in, full_out), 'expert', split_...  87 us
    dot_general x1, matrix products, run_experts(): jnp.einsum('gesd,edf->gesf', shard_piece, weight_in, preferred_element_ty...  28 us
    dot_general x1, matrix products, run_experts(): jnp.einsum('gesf,efd->gesd', hidden, weight_out, preferred_element_type=j...  19.8 us
    reshape x2, local copies, waits for them, and re-layouts, per_device(): outgoing = outgoing.reshape(group_count, local_count, CAP, model_width)  14.2 us
  transfers between devices with their start and end apart: 6, of which 4 were waited for; matrix products, arithmetic and copies ran while one was open for 17% of the time, Pallas kernels for 0%

commit v1 on v0

v1 whole, which is shorter than its diff:
```python
import functools

import jax
import jax.numpy as jnp
from jax import lax
from jax.experimental import pallas as pl
from jax.experimental.pallas import tpu as pltpu
from jax.sharding import PartitionSpec as P

CAP = 20
GROUP = 4


def layer_norm(tokens):
    values = tokens.astype(jnp.float32)
    center = values - jnp.mean(values, axis=-1, keepdims=True)
    spread = jnp.mean(center * center, axis=-1, keepdims=True)
    return (center * lax.rsqrt(spread + 1e-06)).astype(jnp.bfloat16)


def first_kernel(runs, run_tokens, x_ref, key_ref, w_ref, out_ref, rows_ref):
    slots = out_ref.shape[3]
    for j in range(runs):
        span = slice(j * run_tokens, (j + 1) * run_tokens)
        row = lax.broadcasted_iota(jnp.int32, (slots, run_tokens), 0)
        pick = jnp.where(row == key_ref[0, :, span], 1.0, 0.0).astype(jnp.bfloat16)
        rows_ref[j * slots : (j + 1) * slots, :] = jnp.dot(
            pick, x_ref[span, :], preferred_element_type=jnp.float32
        ).astype(jnp.bfloat16)
    pre = jnp.dot(rows_ref[...], w_ref[0], preferred_element_type=jnp.float32)
    for j in range(runs):
        out_ref[j, 0, 0] = pre[j * slots : (j + 1) * slots].astype(jnp.bfloat16)


def first_projection(x, keys, weight, first, count, runs, run_tokens, slots):
    width, hidden = weight.shape[1:]
    chunk = runs * run_tokens
    chunks = x.shape[0] // chunk
    total = count * chunks * runs * slots
    return pl.pallas_call(
        functools.partial(first_kernel, runs, run_tokens),
        grid=(count, chunks),
        in_specs=[
            pl.BlockSpec((chunk, width), lambda e, c: (c, 0)),
            pl.BlockSpec((1, 1, chunk), lambda e, c: (e + first, 0, c)),
            pl.BlockSpec((1, width, hidden), lambda e, c: (e + first, 0, 0)),
        ],
        out_specs=pl.BlockSpec((runs, 1, 1, slots, hidden), lambda e, c: (0, e, c, 0, 0)),
        out_shape=jax.ShapeDtypeStruct((runs, count, chunks, slots, hidden), jnp.bfloat16),
        scratch_shapes=[pltpu.VMEM((runs * slots, width), jnp.bfloat16)],
        cost_estimate=pl.CostEstimate(
            flops=2 * total * width * (hidden + run_tokens),
            bytes_accessed=2 * (count * width * hidden + total * hidden + x.size),
            transcendentals=0,
        ),
    )(x, keys, weight)


def second_kernel(runs, run_tokens, h_ref, key_ref, gate_ref, w_ref, *refs):
    carry_ref, (out_ref, total_ref) = refs[0] if len(refs) == 3 else None, refs[-2:]
    expert = pl.program_id(1)
    slots = h_ref.shape[3]

    @pl.when(expert == 0)
    def _():
        total_ref[...] = jnp.zeros_like(total_ref) if carry_ref is None else carry_ref[...]

    h = jnp.concatenate([h_ref[j, 0, 0] for j in range(runs)], axis=0)
    result = jnp.dot(h, w_ref[0], preferred_element_type=jnp.float32)
    for j in range(runs):
        span = slice(j * run_tokens, (j + 1) * run_tokens)
        row = lax.broadcasted_iota(jnp.int32, (slots, run_tokens), 0)
        match = row == key_ref[0, :, span]
        gate = jnp.sum(jnp.where(match, gate_ref[0, :, span], 0.0), axis=1, keepdims=True)
        scaled = (result[j * slots : (j + 1) * slots] * gate).astype(jnp.bfloat16)
        total_ref[span, :] += lax.dot_general(
            jnp.where(match, 1.0, 0.0).astype(jnp.bfloat16),
            scaled,
            (((0,), (0,)), ((), ())),
            preferred_element_type=jnp.float32,
        )

    @pl.when(expert == pl.num_programs(1) - 1)
    def _():
        out_ref[...] = total_ref[...].astype(out_ref.dtype)


def second_projection(hidden, keys, gates, weight, carry, kind, first, runs, run_tokens):
    _, count, chunks, slots, depth = hidden.shape
    width = weight.shape[2]
    chunk = runs * run_tokens
    total = count * chunks * runs * slots
    carries = [] if carry is None else [carry]
    return pl.pallas_call(
        functools.partial(second_kernel, runs, run_tokens),
        grid=(chunks, count),
        in_specs=[
            pl.BlockSpec((runs, 1, 1, slots, depth), lambda c, e: (0, e, c, 0, 0)),
            pl.BlockSpec((1, 1, chunk), lambda c, e: (e + first, 0, c)),
            pl.BlockSpec((1, 1, chunk), lambda c, e: (e + first, 0, c)),
            pl.BlockSpec((1, depth, width), lambda c, e: (e + first, 0, 0)),
        ]
        + [pl.BlockSpec((chunk, width), lambda c, e: (c, 0)) for _ in carries],
        out_specs=pl.BlockSpec((chunk, width), lambda c, e: (c, 0)),
        out_shape=jax.ShapeDtypeStruct((chunks * chunk, width), kind),
        scratch_shapes=[pltpu.VMEM((chunk, width), jnp.float32)],
        cost_estimate=pl.CostEstimate(
            flops=2 * total * width * (depth + 3 * run_tokens),
            bytes_accessed=2 * (count * depth * width + total * depth) + 4 * chunks * chunk * width,
            transcendentals=0,
        ),
    )(hidden, keys, gates, weight, *carries)


def per_device(tokens, expert_ids, gate_weights, expert_in, expert_out, shared_in, shared_out):
    row_count, model_width = tokens.shape
    pick_count = expert_ids.shape[1]
    local_count = expert_in.shape[0]
    runs = lax.axis_size("dp")
    block_count = runs * lax.axis_size("expert")
    run_tokens = GROUP * row_count
    slots = GROUP * CAP
    halves = 2 if local_count % 2 == 0 else 1

    normed = layer_norm(tokens)
    full_shared_in = lax.all_gather(shared_in, "dp", axis=0, tiled=True)
    full_shared_out = lax.all_gather(shared_out, "dp", axis=1, tiled=True)

    named = jnp.concatenate([expert_ids.astype(jnp.float32), gate_weights], axis=1).T
    named = lax.all_gather(named, ("expert", "dp"), axis=0, tiled=False)
    ids, gates = named[:, :pick_count], named[:, pick_count:]
    columns = lax.all_to_all(normed, "dp", split_axis=1, concat_axis=0, tiled=True)
    x = lax.all_gather(columns, "expert", axis=0, tiled=True)

    owned = lax.axis_index("expert") * local_count + jnp.arange(local_count, dtype=jnp.int32)
    matches = ids[:, :, None, :] == owned.astype(jnp.float32)[:, None]
    chosen = jnp.any(matches, axis=1)
    gate_of = jnp.sum(jnp.where(matches, gates[:, :, None, :], 0.0), axis=1)
    order = jnp.arange(row_count, dtype=jnp.int32)
    before = (order[:, None] < order[None, :]).astype(jnp.bfloat16)
    earlier = jnp.einsum(
        "bej,ji->bei", chosen.astype(jnp.bfloat16), before, preferred_element_type=jnp.float32
    ).astype(jnp.int32)
    base = jnp.arange(block_count, dtype=jnp.int32) % GROUP * CAP
    keys = jnp.where(chosen, earlier + base[:, None, None], -1)

    def by_expert(table):
        return table.transpose(1, 0, 2).reshape(local_count, 1, block_count * row_count)

    keys, gate_of = by_expert(keys), by_expert(gate_of)

    count = local_count // halves
    parts = []
    for half in range(halves):
        pre = first_projection(
            x, keys, expert_in, half * count, count, runs, run_tokens, slots
        )
        parts.append(lax.psum_scatter(pre, "dp", scatter_dimension=0, tiled=True))

    hidden = []
    for pre in parts:
        act = jax.nn.gelu(pre.astype(jnp.float32)).astype(jnp.bfloat16)
        hidden.append(lax.all_gather(act, "dp", axis=0, tiled=True))

    shared_pre = jnp.dot(normed, full_shared_in, preferred_element_type=jnp.float32)
    shared_hidden = jax.nn.gelu(shared_pre).astype(jnp.bfloat16)
    shared_result = jnp.dot(shared_hidden, full_shared_out, preferred_element_type=jnp.float32)

    routed = None
    for half, h in enumerate(hidden):
        kind = jnp.bfloat16 if half == halves - 1 else jnp.float32
        routed = second_projection(
            h, keys, gate_of, expert_out, routed, kind, half * count, runs, run_tokens
        )
    summed = lax.psum_scatter(routed, "expert", scatter_dimension=0, tiled=True)
    own = lax.all_to_all(summed, "dp", split_axis=0, concat_axis=1, tiled=True)
    return (tokens.astype(jnp.float32) + shared_result + own.astype(jnp.float32)).astype(
        jnp.bfloat16
    )


def solution(mesh):
    placed = (
        P(("sweep", "expert", "dp"), None),
        P(("sweep", "expert", "dp"), None),
        P(("sweep", "expert", "dp"), None),
        P(("sweep", "expert"), "dp", None),
        P(("sweep", "expert"), None, "dp"),
        P(("sweep", "dp"), None),
        P("sweep", "dp"),
    )
    return jax.shard_map(
        per_device,
        mesh=mesh,
        in_specs=placed,
        out_specs=P(("sweep", "expert", "dp"), None),
        check_vma=False,
    )
```

time: 625 us -> 336 us (0.54)
  waiting for transfers between devices: 489 us -> 216 us
  local copies, waits for them, and re-layouts: 52.5 us -> 1.53 us
  matrix products: 52.2 us -> 4.4 us
  blocking collectives: 0 us -> 45.4 us
  Pallas kernels: 0 us -> 44.5 us
  starting transfers between devices: 12.1 us -> 0.29 us
    all_gather x4 -> x5, waiting for transfers between devices: 312 us -> 106 us  [the longest x2 52.9 us: per_device(): hidden.append(lax.all_gather(act, 'dp', axis=0, tiled=True))]
    all_to_all x2 -> x0, waiting for transfers between devices: 174 us -> none  [the longest x1 87.2 us: per_device(): lax.all_to_all(outgoing, 'expert', split_axis=0, concat_axis=0, tiled=True)]
    reduce_scatter x0 -> x3, waiting for transfers between devices: none -> 109 us  [the longest x2 74.6 us: per_device(): parts.append(lax.psum_scatter(pre, 'dp', scatter_dimension=0, tiled=True))]
    dot_general x3 -> x2, matrix products: 52.2 us -> 4.4 us  [the longest x1 4.24 us: per_device(): jnp.dot(shared_hidden, full_shared_out, preferred_element_type=jnp.float32)]
    pallas_call x0 -> x4, Pallas kernels: none -> 44.5 us  [the longest x2 24.5 us: second_projection(): pl.pallas_call(functools.partial(second_kernel, runs, run_tokens), grid=(...]
    all_to_all x0 -> x2, blocking collectives: none -> 23.3 us  [the longest x1 11.8 us: per_device(): own = lax.all_to_all(summed, 'dp', split_axis=0, concat_axis=1, tiled=True)]
    all_gather x0 -> x1, blocking collectives: none -> 22.1 us  [per_device(): named = lax.all_gather(named, ('expert', 'dp'), axis=0, tiled=False)]
    reshape x4 -> x0, local copies, waits for them, and re-layouts: 21.3 us -> none  [the longest x2 14.2 us: per_device(): outgoing = outgoing.reshape(group_count, local_count, CAP, model_width)]
  transfers between devices with their start and end apart: 6 -> 8, of which waited for: 4 -> 8; matrix products, arithmetic and copies ran while one was open for 17% -> 2% of each run, Pallas kernels for 0% -> 7%
where the time goes in v1:
time: 336 us; the launch traced here: 335 us
  waiting for transfers between devices  216 us (64%)
  blocking collectives  45.4 us (14%)
  Pallas kernels  44.5 us (13%)
  between operations  13.6 us (4%)
  other arithmetic  9.85 us (3%)
  matrix products  4.4 us (1%)
    reduce_scatter x2, waiting for transfers between devices, per_device(): parts.append(lax.psum_scatter(pre, 'dp', scatter_dimension=0, tiled=True))  74.6 us
    all_gather x2, waiting for transfers between devices, per_device(): hidden.append(lax.all_gather(act, 'dp', axis=0, tiled=True))  52.9 us
    reduce_scatter x1, waiting for transfers between devices, per_device(): summed = lax.psum_scatter(routed, 'expert', scatter_dimension=0, tiled=True)  34.1 us
    all_gather x1, waiting for transfers between devices, per_device(): full_shared_out = lax.all_gather(shared_out, 'dp', axis=1, tiled=True)  25.1 us
    pallas_call x2, Pallas kernels, second_projection(): pl.pallas_call(functools.partial(second_kernel, runs, run_tokens), grid=(...  24.5 us
    all_gather x1, blocking collectives, per_device(): named = lax.all_gather(named, ('expert', 'dp'), axis=0, tiled=False)  22.1 us
    pallas_call x2, Pallas kernels, first_projection(): pl.pallas_call(functools.partial(first_kernel, runs, run_tokens), grid=(c...  20 us
    all_gather x1, waiting for transfers between devices, per_device(): x = lax.all_gather(columns, 'expert', axis=0, tiled=True)  14.5 us
  transfers between devices with their start and end apart: 8, of which 8 were waited for; matrix products, arithmetic and copies ran while one was open for 2% of the time, Pallas kernels for 7%

profile of v1, /device:TPU:0, one launch (start us, length us, event | category | flops | bytes accessed | tf_op | source)
XLA Modules:
  0.0 335.4 jit_solution(1075832449990737262)
XLA Ops:
  6.5 1.2 convert_reduce_fusion
  7.7 1.2 fusion.20
  9.0 1.2 fusion.21
  10.3 11.6 %all_to_all.32 = bf16[128,4,384]{2,0,1:T(8,128)(2,1)} all-to-all(bf16[128,4,384]{2,0,1:T(8,128)(2,1)S(1)} %bitcast.33), channel_id=1, replica_groups=mesh['sweep'=2,'expert'=4,'dp'=4] {'dp'}, dimensions={1} | all-to-all | bytes 786432 | tf_op jit(solution)/shard_map/all_to_all | solution.py:132
  21.8 0.0 reduce-scatter.6.cloned.1.call-start
  21.9 22.1 %all-gather = f32[256,128]{1,0:T(8,128)S(1)} all-gather(f32[16,128]{1,0:T(8,128)S(1)} %maximum_bitcast_fusion), channel_id=2, replica_groups=mesh['sweep'=2,'expert'=4,'dp'=4] {'expert','dp'}, dimensions={0}, use_global_device_ids=true | all-gather | bytes 139264 | tf_op jit(solution)/shard_map/all_gather | solution.py:130
  44.0 0.2 compare_reduce_fusion
  44.2 0.2 fusion.16
  44.4 0.7 copy.15
  45.1 14.5 %all-gather.11.cloned.1.call-done.x_ref = bf16[2048,384]{1,0:T(8,128)(2,1)} async-done(((bf16[512,384]{1,0:T(8,128)(2,1)}), bf16[2048,384]{1,0:T(8,128)(2,1)}) %all-gather.11.cloned.1.call-update) | async-done | bytes 1572880 | tf_op jit(solution)/shard_map/all_gather | solution.py:133
  59.7 9.9 %shard_map.74 = bf16[4,8,1,80,768]{4,3,2,1,0:T(8,128)(2,1)} custom-call(bf16[2048,384]{1,0:T(8,128)(2,1)} %all-gather.11.cloned.1.call-done.x_ref, s32[16,1,2048]{2,1,0:T(1,128)} %bitcast.27, bf16[16,384,768]{2,1,0:T(8,128)(2,1)} %w_ref.5), custom_call_target="tpu_custom_call" | custom-call | flops 2516582400 | bytes 10223616 | tf_op jit(solution)/shard_map/pallas_call | solution.py:40
  69.6 0.0 reduce-scatter.4.cloned.1.call-start
  69.6 10.1 %shard_map.73 = bf16[4,8,1,80,768]{4,3,2,1,0:T(8,128)(2,1)} custom-call(bf16[2048,384]{1,0:T(8,128)(2,1)} %all-gather.11.cloned.1.call-done.x_ref, s32[16,1,2048]{2,1,0:T(1,128)} %bitcast.28, bf16[16,384,768]{2,1,0:T(8,128)(2,1)} %w_ref.5), custom_call_target="tpu_custom_call" | custom-call | flops 2516582400 | bytes 10223616 | tf_op jit(solution)/shard_map/pallas_call | solution.py:40
  79.8 32.1 %reduce-scatter.6.cloned.1.call-done = bf16[1,8,1,80,768]{4,3,2,1,0:T(8,128)(2,1)} async-done(((bf16[4,8,1,80,768]{4,3,2,1,0:T(8,128)(2,1)}), bf16[1,8,1,80,768]{4,3,2,1,0:T(8,128)(2,1)}) %reduce-scatter.6.cloned.1.call-update) | async-done | bytes 983056 | tf_op jit(solution)/shard_map/reduce_scatter | solution.py:158
  111.8 2.9 fusion.13
  114.8 42.5 %reduce-scatter.4.cloned.1.call-done = bf16[1,8,1,80,768]{4,3,2,1,0:T(8,128)(2,1)} async-done(((bf16[4,8,1,80,768]{4,3,2,1,0:T(8,128)(2,1)}), bf16[1,8,1,80,768]{4,3,2,1,0:T(8,128)(2,1)}) %reduce-scatter.4.cloned.1.call-update) | async-done | bytes 983056 | tf_op jit(solution)/shard_map/reduce_scatter | solution.py:158
  157.3 2.8 fusion.7
  160.2 0.2 fusion.17
  160.4 0.7 copy.16
  161.1 30.7 %all-gather.15.cloned.1.call-done.h_ref = bf16[4,8,1,80,768]{4,3,2,1,0:T(8,128)(2,1)} async-done(((bf16[1,8,1,80,768]{4,3,2,1,0:T(8,128)(2,1)}), bf16[4,8,1,80,768]{4,3,2,1,0:T(8,128)(2,1)}) %all-gather.15.cloned.1.call-update) | async-done | bytes 3932176 | tf_op jit(solution)/shard_map/all_gather | solution.py:163
  191.8 12.1 %shard_map.75.refs_0_ = f32[2048,384]{1,0:T(8,128)} custom-call(bf16[4,8,1,80,768]{4,3,2,1,0:T(8,128)(2,1)} %all-gather.15.cloned.1.call-done.h_ref, s32[16,1,2048]{2,1,0:T(1,128)} %bitcast.29, f32[16,1,2048]{2,1,0:T(1,128)} %bitcast.35, bf16[16,768,384]{2,1,0:T(8,128)(2,1)} %w_ref.7), custom_call_target="tpu_custom_call" | custom-call | flops 4529848320 | bytes 11796480 | tf_op jit(solution)/shard_map/pallas_call | solution.py:94
  203.9 22.3 %all-gather.13.cloned.1.call-done.h_ref = bf16[4,8,1,80,768]{4,3,2,1,0:T(8,128)(2,1)} async-done(((bf16[1,8,1,80,768]{4,3,2,1,0:T(8,128)(2,1)}), bf16[4,8,1,80,768]{4,3,2,1,0:T(8,128)(2,1)}) %all-gather.13.cloned.1.call-update) | async-done | bytes 3932176 | tf_op jit(solution)/shard_map/all_gather | solution.py:163
  226.2 12.4 %shard_map.76 = bf16[2048,384]{1,0:T(8,128)(2,1)} custom-call(bf16[4,8,1,80,768]{4,3,2,1,0:T(8,128)(2,1)} %all-gather.13.cloned.1.call-done.h_ref, s32[16,1,2048]{2,1,0:T(1,128)} %bitcast.30, f32[16,1,2048]{2,1,0:T(1,128)} %bitcast.36, bf16[16,768,384]{2,1,0:T(8,128)(2,1)} %w_ref.7, f32[2048,384]{1,0:T(8,128)} %shard_map.75.refs_0_), custom_call_target="tpu_custom_call" | custom-call | flops 4529848320 | bytes 11796480 | tf_op jit(solution)/shard_map/pallas_call | solution.py:94
  238.7 0.7 all-gather.7.cloned.1.call-update
  239.4 0.7 all-gather.9.cloned.1.call-update
  240.1 34.1 %reduce-scatter.8.cloned.1.call-done = bf16[512,384]{1,0:T(8,128)(2,1)} async-done(((bf16[2048,384]{1,0:T(8,128)(2,1)}), bf16[512,384]{1,0:T(8,128)(2,1)}) %reduce-scatter.8.cloned.1.call-update) | async-done | bytes 393232 | tf_op jit(solution)/shard_map/reduce_scatter | solution.py:175
  274.2 11.8 %all_to_all.33 = bf16[4,128,384]{2,1,0:T(8,128)(2,1)S(1)} all-to-all(bf16[4,128,384]{2,1,0:T(8,128)(2,1)} %bitcast.39), channel_id=1, replica_groups=mesh['sweep'=2,'expert'=4,'dp'=4] {'dp'}, dimensions={0} | all-to-all | bytes 786432 | tf_op jit(solution)/shard_map/all_to_all | solution.py:176
  286.0 0.1 convert_bitcast_fusion
  286.0 0.1 copy.19
  286.1 13.1 %all-gather.7.cloned.1.call-done = bf16[1536,768]{1,0:T(8,128)(2,1)} async-done(((bf16[384,768]{1,0:T(8,128)(2,1)}), bf16[1536,768]{1,0:T(8,128)(2,1)}) %all-gather.7.cloned.1.call-update) | async-done | bytes 2359312 | tf_op jit(solution)/shard_map/all_gather | solution.py:126
  299.2 25.1 %all-gather.9.cloned.1.call-done = bf16[768,1536]{1,0:T(8,128)(2,1)} async-done(((bf16[768,384]{1,0:T(8,128)(2,1)}), bf16[768,1536]{1,0:T(8,128)(2,1)}) %all-gather.9.cloned.1.call-update) | async-done | bytes 2359312 | tf_op jit(solution)/shard_map/all_gather | solution.py:127
  324.3 4.2 %fusion.1 = bf16[128,1536]{1,0:T(8,128)(2,1)} fusion(f32[128,1536]{1,0:T(8,128)S(1)} %bitcast.31, bf16[768,1536]{1,0:T(8,128)(2,1)} %all-gather.9.cloned.1.call-done, bf16[128,1536]{1,0:T(8,128)(2,1)S(1)} %copy-done, bf16[1536,768]{1,0:T(8,128)(2,1)} %all-gather.7.cloned.1.call-done, f32[128]{0:T(128)S(1)} %add_rsqrt_fusion, f32[128]{0:T(128)S(1)} %broadcast_multiply_fusion), kind=kOutput, calls=%fused_computation.10 | convolution fusion | flops 606437376 | bytes 6292480 | tf_op jit(solution)/shard_map/dot_general | solution.py:167
  (26 shorter events, 0.4 us)
Async XLA Ops:
  6.5 15.3 %copy-start.1 = (s32[128,8]{0,1:T(8,128)S(1)}, s32[128,8]{0,1:T(8,128)}, u32[]{:S(2)}) copy-start(s32[128,8]{0,1:T(8,128)} %param.8) | copy-start | bytes 12292
  6.5 15.4 %copy-start.2 = (f32[128,8]{0,1:T(8,128)S(1)}, f32[128,8]{0,1:T(8,128)}, u32[]{:S(2)}) copy-start(f32[128,8]{0,1:T(8,128)} %param.9) | copy-start | bytes 12292
  6.5 53.1 %all-gather.11.cloned.1.call-start = ((), (), s32[]{:S(2)}) async-start(), calls=%async_computation.7 | async-start | bytes 1966080 | tf_op jit(solution)/shard_map/all_gather | solution.py:133
  21.8 90.0 %reduce-scatter.6.cloned.1.call-start = ((), (), s32[]{:S(2)}) async-start(), calls=%async_computation.10 | async-start | bytes 4915200 | tf_op jit(solution)/shard_map/reduce_scatter | solution.py:158
  69.6 87.8 %reduce-scatter.4.cloned.1.call-start = ((), (), s32[]{:S(2)}) async-start(), calls=%async_computation.8 | async-start | bytes 4915200 | tf_op jit(solution)/shard_map/reduce_scatter | solution.py:158
  79.7 112.0 %all-gather.15.cloned.1.call-start = ((), (), s32[]{:S(2)}) async-start(), calls=%async_computation.11 | async-start | bytes 4915200 | tf_op jit(solution)/shard_map/all_gather | solution.py:163
  114.8 111.4 %all-gather.13.cloned.1.call-start = ((), (), s32[]{:S(2)}) async-start(), calls=%async_computation.9 | async-start | bytes 4915200 | tf_op jit(solution)/shard_map/all_gather | solution.py:163
  160.2 114.0 %reduce-scatter.8.cloned.1.call-start = ((), (), s32[]{:S(2)}) async-start(), calls=%async_computation.12 | async-start | bytes 1966080 | tf_op jit(solution)/shard_map/reduce_scatter | solution.py:175
  238.6 60.6 %all-gather.7.cloned.1.call-start = ((), (), s32[]{:S(2)}) async-start(), calls=%async_computation.5 | async-start | bytes 2949120 | tf_op jit(solution)/shard_map/all_gather | solution.py:126
  239.4 84.9 %copy-start = (bf16[128,1536]{1,0:T(8,128)(2,1)S(1)}, bf16[128,1536]{1,0:T(8,128)(2,1)}, u32[]{:S(2)}) copy-start(bf16[128,1536]{1,0:T(8,128)(2,1)} %param.7) | copy-start | bytes 1179652
  239.4 84.9 %all-gather.9.cloned.1.call-start = ((), (), s32[]{:S(2)}) async-start(), calls=%async_computation.6 | async-start | bytes 2949120 | tf_op jit(solution)/shard_map/all_gather | solution.py:127
Sparse Core Ops, SparseCore 0:
  21.9 37.6 all-gather.10
  69.7 42.1 reduce-scatter.5
  114.4 42.9 reduce-scatter.3
  158.8 32.9 all-gather.14
  193.2 32.9 all-gather.12
  238.7 35.4 reduce-scatter.7
  275.8 23.4 all-gather.6
  300.8 23.4 all-gather.8
